TPU v7x, 128 devices: a whole 4x4x4 slice. The times are simulated.
128 devices in a mesh: fsdp: 32 (over x_hi, z, y), tensor: 4 (over x_lo, core).
Axes of the slice: x: 4 (x_hi: 2, x_lo: 2; x = x_hi * 2 + x_lo), y: 4, z: 4, core: 2. Of those that a mesh axis runs over, the one named last changes fastest.
Arguments:
- activations: bfloat16 [32768, 5120], P('fsdp', 'tensor'), may hold values from -6 to 6
- cotangent: bfloat16 [32768, 5120], P('fsdp', 'tensor'), may hold values from -0.032958984 to 0.032958984
- weights: float32 [5120, 5120], P(None, ('tensor', 'fsdp')), may hold values from -0.025 to 0.025
- first_moment: float32 [5120, 5120], P(None, ('tensor', 'fsdp')), may hold values from -3 to 3
- second_moment: float32 [5120, 5120], P(None, ('tensor', 'fsdp')), may hold values from 0.01 to 1
Outputs:
- weights_new: float32 [5120, 5120], P('fsdp', 'tensor')
- first_new: float32 [5120, 5120], P('fsdp', 'tensor')
- second_new: float32 [5120, 5120], P('fsdp', 'tensor')
- weights_bf16: bfloat16 [5120, 5120], P(None, 'tensor')
All inputs are finite; a program needn't handle non-finite values.
Results may differ from a plain program's by a relative error of at most 0.014.
Values may be sent and summed in bfloat16 or wider, within the bound.
No kernel may reach another device: no remote copies, remote signals or barrier semaphores. Data moves between devices by JAX's collectives and lax.ppermute only.
A program may use at most 128 MiB of HBM per device.

v0:
```python
import jax
import jax.numpy as jnp
from jax import lax
from jax.sharding import PartitionSpec as P

STEP = 20
beta_one = 0.9
beta_two = 0.95
adam_eps = 1e-08
learn_rate = 0.0003
decay_rate = 0.1


def split_up(value, dim, count):
    before, after = (value.shape[:dim], value.shape[dim + 1 :])
    return jnp.moveaxis(value.reshape(*before, count, -1, *after), dim, 0)


def sent_and_summed(value, axis, dim):
    count = lax.axis_size(axis)
    parts = lax.all_to_all(split_up(value, dim, count), axis, 0, 0, tiled=True)
    return jnp.sum(parts.astype(jnp.float32), axis=0)


def adam_update(weights, first_moment, second_moment, gradient):
    first_new = beta_one * first_moment + (1.0 - beta_one) * gradient
    second_new = beta_two * second_moment + (1.0 - beta_two) * gradient * gradient
    corrected = first_new / (1.0 - beta_one**STEP)
    scaled = jnp.sqrt(second_new / (1.0 - beta_two**STEP)) + adam_eps
    weights_new = weights - learn_rate * (corrected / scaled + decay_rate * weights)
    return (weights_new, first_new, second_new)


def body(activations, cotangent, weights, first_moment, second_moment):
    gathered = lax.all_gather(activations, "tensor", axis=1, tiled=True)
    transposed = sent_and_summed(
        lax.dot_general(
            cotangent, gathered, (((0,), (0,)), ((), ())), preferred_element_type=jnp.float32
        ).astype(jnp.bfloat16),
        "fsdp",
        0,
    )
    gradient = transposed.T
    weights_old, first_old, second_old = adam_update(weights, first_moment, second_moment, gradient)
    weights_bf16 = lax.all_gather(weights_old.astype(jnp.bfloat16), "fsdp", axis=1, tiled=True)
    weights_new, first_new, second_new = (
        lax.all_to_all(
            weights_old.astype(jnp.bfloat16), "fsdp", split_axis=0, concat_axis=1, tiled=True
        ).astype(weights_old.dtype),
        lax.all_to_all(
            first_old.astype(jnp.bfloat16), "fsdp", split_axis=0, concat_axis=1, tiled=True
        ).astype(first_old.dtype),
        lax.all_to_all(
            second_old.astype(jnp.bfloat16), "fsdp", split_axis=0, concat_axis=1, tiled=True
        ).astype(second_old.dtype),
    )
    return (weights_new, first_new, second_new, weights_bf16)


def solution(mesh):
    return jax.shard_map(
        body,
        mesh=mesh,
        in_specs=(
            P("fsdp", "tensor"),
            P("fsdp", "tensor"),
            P(None, ("tensor", "fsdp")),
            P(None, ("tensor", "fsdp")),
            P(None, ("tensor", "fsdp")),
        ),
        out_specs=(
            P("fsdp", "tensor"),
            P("fsdp", "tensor"),
            P("fsdp", "tensor"),
            P(None, "tensor"),
        ),
        check_vma=False,
    )
```

profile of v0, /device:TPU:0, one launch (start us, length us, event | category | flops | bytes accessed | tf_op | source)
XLA Modules:
  0.0 469.7 jit_solution(9544911949169199346)
XLA Ops:
  7.2 0.0 copy-start
  7.2 0.0 all-gather.3.cloned.1.call-start
  7.2 0.7 all-gather.3.cloned.1.call-update
  7.9 0.0 all-gather.5.cloned.1.call-start
  8.0 101.3 %all-gather.3.cloned.1.call-done = bf16[1024,5120]{1,0:T(8,128)(2,1)} async-done(((bf16[1024,1280]{1,0:T(8,128)(2,1)}), bf16[1024,5120]{1,0:T(8,128)(2,1)}) %all-gather.3.cloned.1.call-update) | async-done | bytes 10485776 | tf_op jit(solution)/shard_map/all_gather | solution.py:35
  109.3 20.2 %convolution_convert_fusion = bf16[1280,5120]{1,0:T(8,128)(2,1)} fusion(bf16[1024,1280]{1,0:T(8,128)(2,1)S(1)} %copy-done, bf16[1024,5120]{1,0:T(8,128)(2,1)} %all-gather.3.cloned.1.call-done), kind=kOutput, calls=%fused_computation.1 | convolution fusion | flops 13428326400 | bytes 26214400 | tf_op jit(solution)/shard_map/dot_general | solution.py:37
  129.5 158.0 %all_to_all.44 = bf16[32,40,5120]{2,1,0:T(8,128)(2,1)} all-to-all(bf16[32,40,5120]{2,1,0:T(8,128)(2,1)} %bitcast.31), channel_id=1, replica_groups=mesh['fsdp'=32,'tensor'=4] {'fsdp'}, dimensions={0} | all-to-all | bytes 26214400 | tf_op jit(solution)/shard_map/all_to_all | solution.py:21
  287.4 7.7 %convert_reduce_fusion = f32[40,5120]{1,0:T(8,128)S(1)} fusion(bf16[32,40,5120]{2,1,0:T(8,128)(2,1)} %all_to_all.44), kind=kLoop, calls=%fused_computation | loop fusion | flops 12902400 | bytes 13926400 | tf_op jit(solution)/shard_map/reduce_sum | solution.py:22
  295.1 0.0 copy-done.2
  295.1 0.0 copy-done.3
  295.1 2.6 fusion.3
  297.7 0.0 all-gather.5.cloned.1.call-update
  297.7 0.8 all_to_all.38
  298.5 1.2 copy.28
  299.7 7.0 %all-to-all-start.3 = ((bf16[32,160,40]{1,2,0:T(8,128)(2,1)}), bf16[32,160,40]{1,2,0:T(8,128)(2,1)S(1)}, u32[]{:S(2)}, u32[]{:S(2)}) async-start(bf16[32,160,40]{1,2,0:T(8,128)(2,1)} %copy.28), calls=%async_computation.3 | async-start | bytes 1310720 | tf_op jit(solution)/shard_map/all_to_all | solution.py:53
  306.8 0.8 all_to_all.36
  307.6 1.2 copy.27
  308.8 13.6 %all-to-all-done.3 = bf16[32,160,40]{1,2,0:T(8,128)(2,1)S(1)} async-done(((bf16[32,160,40]{1,2,0:T(8,128)(2,1)}), bf16[32,160,40]{1,2,0:T(8,128)(2,1)S(1)}, u32[]{:S(2)}, u32[]{:S(2)}) %all-to-all-start.3) | async-done | bytes 409632 | tf_op jit(solution)/shard_map/all_to_all | solution.py:53
  322.4 4.7 %all-to-all-start.2 = ((bf16[32,160,40]{1,2,0:T(8,128)(2,1)}), bf16[32,160,40]{1,2,0:T(8,128)(2,1)S(1)}, u32[]{:S(2)}, u32[]{:S(2)}) async-start(bf16[32,160,40]{1,2,0:T(8,128)(2,1)} %copy.27), calls=%async_computation.2 | async-start | bytes 1310720 | tf_op jit(solution)/shard_map/all_to_all | solution.py:50
  327.1 1.8 all_to_all.34
  328.9 1.2 copy.26
  330.1 10.4 %all-to-all-done.2 = bf16[32,160,40]{1,2,0:T(8,128)(2,1)S(1)} async-done(((bf16[32,160,40]{1,2,0:T(8,128)(2,1)}), bf16[32,160,40]{1,2,0:T(8,128)(2,1)S(1)}, u32[]{:S(2)}, u32[]{:S(2)}) %all-to-all-start.2) | async-done | bytes 409632 | tf_op jit(solution)/shard_map/all_to_all | solution.py:50
  340.5 4.0 all-to-all-start.1
  344.5 0.1 convert_element_type.62
  344.6 1.3 copy.31
  345.9 0.1 convert_element_type.61
  346.0 1.3 copy.30
  347.2 16.4 %all-to-all-done.1 = bf16[32,160,40]{1,2,0:T(8,128)(2,1)S(1)} async-done(((bf16[32,160,40]{1,2,0:T(8,128)(2,1)}), bf16[32,160,40]{1,2,0:T(8,128)(2,1)S(1)}, u32[]{:S(2)}, u32[]{:S(2)}) %all-to-all-start.1) | async-done | bytes 409632 | tf_op jit(solution)/shard_map/all_to_all | solution.py:47
  363.6 1.2 convert_element_type.60
  364.8 2.7 copy.29
  367.5 77.8 %all-gather.5.cloned.1.call-done = bf16[5120,1280]{0,1:T(8,128)(2,1)} async-done(((bf16[5120,40]{0,1:T(8,128)(2,1)}), bf16[5120,1280]{0,1:T(8,128)(2,1)}) %all-gather.5.cloned.1.call-update) | async-done | bytes 13107216 | tf_op jit(solution)/shard_map/all_gather | solution.py:45
  445.3 17.6 %copy.32 = bf16[5120,1280]{1,0:T(8,128)(2,1)} copy(bf16[5120,1280]{0,1:T(8,128)(2,1)} %all-gather.5.cloned.1.call-done) | data formatting | bytes 26214400
  (5 shorter events, 0.0 us)
Async XLA Ops:
  7.2 102.1 %copy-start = (bf16[1024,1280]{1,0:T(8,128)(2,1)S(1)}, bf16[1024,1280]{1,0:T(8,128)(2,1)}, u32[]{:S(2)}) copy-start(bf16[1024,1280]{1,0:T(8,128)(2,1)} %param.6) | copy-start | bytes 7864324
  7.2 102.1 %all-gather.3.cloned.1.call-start = ((), (), s32[]{:S(2)}) async-start(), calls=%async_computation.4 | async-start | bytes 13107200 | tf_op jit(solution)/shard_map/all_gather | solution.py:35
  7.9 437.4 %all-gather.5.cloned.1.call-start = ((), (), s32[]{:S(2)}) async-start(), calls=%async_computation.5 | async-start | bytes 13516800 | tf_op jit(solution)/shard_map/all_gather | solution.py:45
  287.4 7.7 %copy-start.2 = (f32[5120,40]{0,1:T(8,128)S(1)}, f32[5120,40]{0,1:T(8,128)}, u32[]{:S(2)}) copy-start(f32[5120,40]{0,1:T(8,128)} %param.9) | copy-start | bytes 2457604
  287.4 7.7 %copy-start.3 = (f32[5120,40]{0,1:T(8,128)S(1)}, f32[5120,40]{0,1:T(8,128)}, u32[]{:S(2)}) copy-start(f32[5120,40]{0,1:T(8,128)} %param.7) | copy-start | bytes 2457604
  299.7 22.6 %all-to-all-start.3 = ((bf16[32,160,40]{1,2,0:T(8,128)(2,1)}), bf16[32,160,40]{1,2,0:T(8,128)(2,1)S(1)}, u32[]{:S(2)}, u32[]{:S(2)}) async-start(bf16[32,160,40]{1,2,0:T(8,128)(2,1)} %copy.28), calls=%async_computation.3 | async-start | bytes 1310720 | tf_op jit(solution)/shard_map/all_to_all | solution.py:53
  322.4 18.1 %all-to-all-start.2 = ((bf16[32,160,40]{1,2,0:T(8,128)(2,1)}), bf16[32,160,40]{1,2,0:T(8,128)(2,1)S(1)}, u32[]{:S(2)}, u32[]{:S(2)}) async-start(bf16[32,160,40]{1,2,0:T(8,128)(2,1)} %copy.27), calls=%async_computation.2 | async-start | bytes 1310720 | tf_op jit(solution)/shard_map/all_to_all | solution.py:50
  340.5 23.1 %all-to-all-start.1 = ((bf16[32,160,40]{1,2,0:T(8,128)(2,1)}), bf16[32,160,40]{1,2,0:T(8,128)(2,1)S(1)}, u32[]{:S(2)}, u32[]{:S(2)}) async-start(bf16[32,160,40]{1,2,0:T(8,128)(2,1)} %copy.26), calls=%async_computation.1 | async-start | bytes 1310720 | tf_op jit(solution)/shard_map/all_to_all | solution.py:47
  364.8 98.1 %copy-start.1 = (bf16[1024,1280]{1,0:T(8,128)(2,1)S(1)}, bf16[1024,1280]{1,0:T(8,128)(2,1)}, u32[]{:S(2)}) copy-start(bf16[1024,1280]{1,0:T(8,128)(2,1)} %param.6) | copy-start | bytes 7864324
Sparse Core Ops, SparseCore 0:
  9.6 99.5 all-gather.2
  297.8 147.3 all-gather.4
where the time goes:
time: 471 us; the launch traced here: 470 us
  waiting for transfers between devices  220 us (47%)
  blocking collectives  158 us (34%)
  local copies, waits for them, and re-layouts  29.9 us (6%)
  matrix products  20.2 us (4%)
  starting transfers between devices  15.8 us (3%)
  between operations  14.1 us (3%)
  other arithmetic  11.6 us (2%)
    all_to_all x1, blocking collectives, sent_and_summed(): parts = lax.all_to_all(split_up(value, dim, count), axis, 0, 0, tiled=True)  158 us
    all_gather x1, waiting for transfers between devices, body(): gathered = lax.all_gather(activations, 'tensor', axis=1, tiled=True)  101 us
    all_gather x1, waiting for transfers between devices, body(): lax.all_gather(weights_old.astype(jnp.bfloat16), 'fsdp', axis=1, tiled=True)  77.8 us
    unnamed x12, local copies, waits for them, and re-layouts  22.9 us
    dot_general x1, matrix products, body(): lax.dot_general(cotangent, gathered, (((0,), (0,)), ((), ())), preferred_...  20.2 us
    all_to_all x1, waiting for transfers between devices, body(): lax.all_to_all(weights_old.astype(jnp.bfloat16), 'fsdp', split_axis=0, co...  16.4 us
    all_to_all x1, waiting for transfers between devices, body(): lax.all_to_all(second_old.astype(jnp.bfloat16), 'fsdp', split_axis=0, con...  13.6 us
    all_to_all x1, waiting for transfers between devices, body(): lax.all_to_all(first_old.astype(jnp.bfloat16), 'fsdp', split_axis=0, conc...  10.4 us
  transfers between devices with their start and end apart: 5, of which 5 were waited for; matrix products, arithmetic and copies ran while one was open for 2% of the time, Pallas kernels for 0%

commit v1 on v0

--- a/solution.py
+++ b/solution.py
@@ -32,7 +32,7 @@
 
 
 def body(activations, cotangent, weights, first_moment, second_moment):
-    gathered = lax.all_gather(activations, "tensor", axis=1, tiled=True)
+    gathered = jnp.concatenate(lax.all_gather(activations, "tensor"), axis=1)
     transposed = sent_and_summed(
         lax.dot_general(
             cotangent, gathered, (((0,), (0,)), ((), ())), preferred_element_type=jnp.float32

time: 471 us -> 486 us (1.032)
  local copies, waits for them, and re-layouts: 29.9 us -> 44.3 us
    reshape x0 -> x1, local copies, waits for them, and re-layouts: none -> 14.4 us  [body(): gathered = jnp.concatenate(lax.all_gather(activations, 'tensor'), axis=1)]
where the time goes in v1:
time: 486 us; the launch traced here: 484 us
  waiting for transfers between devices  217 us (45%)
  blocking collectives  158 us (33%)
  local copies, waits for them, and re-layouts  44.3 us (9%)
  matrix products  20.5 us (4%)
  starting transfers between devices  18.7 us (4%)
  between operations  14.1 us (3%)
  other arithmetic  11.6 us (2%)
    all_to_all x1, blocking collectives, sent_and_summed(): parts = lax.all_to_all(split_up(value, dim, count), axis, 0, 0, tiled=True)  158 us
    all_gather x1, waiting for transfers between devices, body(): gathered = jnp.concatenate(lax.all_gather(activations, 'tensor'), axis=1)  101 us
    all_gather x1, waiting for transfers between devices, body(): lax.all_gather(weights_old.astype(jnp.bfloat16), 'fsdp', axis=1, tiled=True)  77.6 us
    unnamed x12, local copies, waits for them, and re-layouts  22.9 us
    dot_general x1, matrix products, body(): lax.dot_general(cotangent, gathered, (((0,), (0,)), ((), ())), preferred_...  20.5 us
    all_to_all x1, waiting for transfers between devices, body(): lax.all_to_all(second_old.astype(jnp.bfloat16), 'fsdp', split_axis=0, con...  15.6 us
    reshape x1, local copies, waits for them, and re-layouts, body(): gathered = jnp.concatenate(lax.all_gather(activations, 'tensor'), axis=1)  14.4 us
    all_to_all x1, waiting for transfers between devices, body(): lax.all_to_all(weights_old.astype(jnp.bfloat16), 'fsdp', split_axis=0, co...  12.3 us
  transfers between devices with their start and end apart: 5, of which 5 were waited for; matrix products, arithmetic and copies ran while one was open for 2% of the time, Pallas kernels for 0%

profile of v1, /device:TPU:0, one launch (start us, length us, event | category | flops | bytes accessed | tf_op | source)
XLA Modules:
  0.0 484.4 jit_solution(18147997051075165703)
XLA Ops:
  7.2 0.0 copy-start
  7.2 0.0 all-gather.6.cloned.1.call-start
  7.2 0.7 all-gather.6.cloned.1.call-update
  7.9 0.0 all-gather.4.cloned.1.call-start
  8.0 101.3 %all-gather.6.cloned.1.call-done = bf16[4096,1280]{1,0:T(8,128)(2,1)} async-done(((bf16[1024,1280]{1,0:T(8,128)(2,1)}), bf16[4096,1280]{1,0:T(8,128)(2,1)}) %all-gather.6.cloned.1.call-update) | async-done | bytes 10485776 | tf_op jit(solution)/shard_map/all_gather | solution.py:35
  109.3 14.4 %copy.37 = bf16[1024,4,1280]{0,2,1:T(8,128)(2,1)} copy(bf16[1024,4,1280]{2,0,1:T(8,128)(2,1)} %bitcast.36) | data formatting | bytes 20971520 | tf_op jit(solution)/shard_map/reshape | solution.py:35
  123.7 20.5 %convolution_convert_fusion = bf16[1280,5120]{1,0:T(8,128)(2,1)} fusion(bf16[1024,1280]{1,0:T(8,128)(2,1)S(1)} %copy-done, bf16[1024,5120]{0,1:T(8,128)(2,1)} %bitcast.37), kind=kOutput, calls=%fused_computation.1 | convolution fusion | flops 13428326400 | bytes 26214400 | tf_op jit(solution)/shard_map/dot_general | solution.py:37
  144.2 158.0 %all_to_all.44 = bf16[32,40,5120]{2,1,0:T(8,128)(2,1)} all-to-all(bf16[32,40,5120]{2,1,0:T(8,128)(2,1)} %bitcast.35), channel_id=1, replica_groups=mesh['fsdp'=32,'tensor'=4] {'fsdp'}, dimensions={0} | all-to-all | bytes 26214400 | tf_op jit(solution)/shard_map/all_to_all | solution.py:21
  302.2 7.7 %convert_reduce_fusion = f32[40,5120]{1,0:T(8,128)S(1)} fusion(bf16[32,40,5120]{2,1,0:T(8,128)(2,1)} %all_to_all.44), kind=kLoop, calls=%fused_computation | loop fusion | flops 12902400 | bytes 13926400 | tf_op jit(solution)/shard_map/reduce_sum | solution.py:22
  309.8 2.6 fusion.3
  312.4 0.0 all-gather.4.cloned.1.call-update
  312.4 0.8 all_to_all.38
  313.3 1.2 copy.40
  314.5 10.4 %all-to-all-start.3 = ((bf16[32,160,40]{1,2,0:T(8,128)(2,1)}), bf16[32,160,40]{1,2,0:T(8,128)(2,1)S(1)}, u32[]{:S(2)}, u32[]{:S(2)}) async-start(bf16[32,160,40]{1,2,0:T(8,128)(2,1)} %copy.40), calls=%async_computation.3 | async-start | bytes 1310720 | tf_op jit(solution)/shard_map/all_to_all | solution.py:53
  324.9 0.8 all_to_all.36
  325.7 1.2 copy.39
  326.9 15.6 %all-to-all-done.3 = bf16[32,160,40]{1,2,0:T(8,128)(2,1)S(1)} async-done(((bf16[32,160,40]{1,2,0:T(8,128)(2,1)}), bf16[32,160,40]{1,2,0:T(8,128)(2,1)S(1)}, u32[]{:S(2)}, u32[]{:S(2)}) %all-to-all-start.3) | async-done | bytes 409632 | tf_op jit(solution)/shard_map/all_to_all | solution.py:53
  342.5 4.1 all-to-all-start.2
  346.7 1.8 all_to_all.34
  348.5 1.2 copy.38
  349.7 9.6 %all-to-all-done.2 = bf16[32,160,40]{1,2,0:T(8,128)(2,1)S(1)} async-done(((bf16[32,160,40]{1,2,0:T(8,128)(2,1)}), bf16[32,160,40]{1,2,0:T(8,128)(2,1)S(1)}, u32[]{:S(2)}, u32[]{:S(2)}) %all-to-all-start.2) | async-done | bytes 409632 | tf_op jit(solution)/shard_map/all_to_all | solution.py:50
  359.3 4.1 all-to-all-start.1
  363.4 0.1 convert_element_type.62
  363.5 1.3 copy.43
  364.8 0.1 convert_element_type.61
  364.9 1.3 copy.42
  366.2 12.3 %all-to-all-done.1 = bf16[32,160,40]{1,2,0:T(8,128)(2,1)S(1)} async-done(((bf16[32,160,40]{1,2,0:T(8,128)(2,1)}), bf16[32,160,40]{1,2,0:T(8,128)(2,1)S(1)}, u32[]{:S(2)}, u32[]{:S(2)}) %all-to-all-start.1) | async-done | bytes 409632 | tf_op jit(solution)/shard_map/all_to_all | solution.py:47
  378.5 1.2 convert_element_type.60
  379.6 2.7 copy.41
  382.3 77.6 %all-gather.4.cloned.1.call-done = bf16[5120,1280]{0,1:T(8,128)(2,1)} async-done(((bf16[5120,40]{0,1:T(8,128)(2,1)}), bf16[5120,1280]{0,1:T(8,128)(2,1)}) %all-gather.4.cloned.1.call-update) | async-done | bytes 13107216 | tf_op jit(solution)/shard_map/all_gather | solution.py:45
  460.0 17.6 %copy.44 = bf16[5120,1280]{1,0:T(8,128)(2,1)} copy(bf16[5120,1280]{0,1:T(8,128)(2,1)} %all-gather.4.cloned.1.call-done) | data formatting | bytes 26214400
  477.6 0.0 copy-done.1
  (6 shorter events, 0.0 us)
Async XLA Ops:
  7.2 116.5 %copy-start = (bf16[1024,1280]{1,0:T(8,128)(2,1)S(1)}, bf16[1024,1280]{1,0:T(8,128)(2,1)}, u32[]{:S(2)}) copy-start(bf16[1024,1280]{1,0:T(8,128)(2,1)} %param.6) | copy-start | bytes 7864324
  7.2 102.1 %all-gather.6.cloned.1.call-start = ((), (), s32[]{:S(2)}) async-start(), calls=%async_computation.5 | async-start | bytes 13107200 | tf_op jit(solution)/shard_map/all_gather | solution.py:35
  7.9 452.1 %all-gather.4.cloned.1.call-start = ((), (), s32[]{:S(2)}) async-start(), calls=%async_computation.4 | async-start | bytes 13516800 | tf_op jit(solution)/shard_map/all_gather | solution.py:45
  302.2 7.7 %copy-start.2 = (f32[5120,40]{0,1:T(8,128)S(1)}, f32[5120,40]{0,1:T(8,128)}, u32[]{:S(2)}) copy-start(f32[5120,40]{0,1:T(8,128)} %param.9) | copy-start | bytes 2457604
  302.2 7.7 %copy-start.3 = (f32[5120,40]{0,1:T(8,128)S(1)}, f32[5120,40]{0,1:T(8,128)}, u32[]{:S(2)}) copy-start(f32[5120,40]{0,1:T(8,128)} %param.7) | copy-start | bytes 2457604
  314.5 28.0 %all-to-all-start.3 = ((bf16[32,160,40]{1,2,0:T(8,128)(2,1)}), bf16[32,160,40]{1,2,0:T(8,128)(2,1)S(1)}, u32[]{:S(2)}, u32[]{:S(2)}) async-start(bf16[32,160,40]{1,2,0:T(8,128)(2,1)} %copy.40), calls=%async_computation.3 | async-start | bytes 1310720 | tf_op jit(solution)/shard_map/all_to_all | solution.py:53
  342.5 16.8 %all-to-all-start.2 = ((bf16[32,160,40]{1,2,0:T(8,128)(2,1)}), bf16[32,160,40]{1,2,0:T(8,128)(2,1)S(1)}, u32[]{:S(2)}, u32[]{:S(2)}) async-start(bf16[32,160,40]{1,2,0:T(8,128)(2,1)} %copy.39), calls=%async_computation.2 | async-start | bytes 1310720 | tf_op jit(solution)/shard_map/all_to_all | solution.py:50
  359.3 19.2 %all-to-all-start.1 = ((bf16[32,160,40]{1,2,0:T(8,128)(2,1)}), bf16[32,160,40]{1,2,0:T(8,128)(2,1)S(1)}, u32[]{:S(2)}, u32[]{:S(2)}) async-start(bf16[32,160,40]{1,2,0:T(8,128)(2,1)} %copy.38), calls=%async_computation.1 | async-start | bytes 1310720 | tf_op jit(solution)/shard_map/all_to_all | solution.py:47
  379.6 98.0 %copy-start.1 = (bf16[1024,1280]{1,0:T(8,128)(2,1)S(1)}, bf16[1024,1280]{1,0:T(8,128)(2,1)}, u32[]{:S(2)}) copy-start(bf16[1024,1280]{1,0:T(8,128)(2,1)} %param.6) | copy-start | bytes 7864324
Sparse Core Ops, SparseCore 0:
  9.6 99.5 all-gather.5
  312.6 147.3 all-gather.3
